TPU v7x, 512 devices: a whole 4x4x16 slice. The times are simulated.
512 devices in a mesh: gx: 32 (over z, x_lo), gy: 16 (over y, x_hi, core).
Axes of the slice: x: 4 (x_hi: 2, x_lo: 2; x = x_hi * 2 + x_lo), y: 4, z: 16, core: 2. Of those that a mesh axis runs over, the one named last changes fastest.
Arguments:
- field: float32 [256, 128, 192], P('gx', 'gy'), may hold values from -6 to 6
- target: float32 [256, 128, 192], P('gx', 'gy'), may hold values from -6 to 6
- embed_weight: float32 [192, 256], replicated, may hold values from -0.4375 to 0.4375
- norm_gain: float32 [256], replicated, may hold values from 0.5 to 1.5
- attend_weight: float32 [256, 768], replicated, may hold values from -0.375 to 0.375
- output_weight: float32 [256, 256], replicated, may hold values from -0.375 to 0.375
- second_gain: float32 [256], replicated, may hold values from 0.5 to 1.5
- expand_weight: float32 [256, 512], replicated, may hold values from -0.375 to 0.375
- reduce_weight: float32 [512, 256], replicated, may hold values from -0.25 to 0.25
- decode_weight: float32 [256, 192], replicated, may hold values from -0.375 to 0.375
Outputs:
- loss: float32 [], replicated
- field_gradient: float32 [256, 128, 192], P('gx', 'gy')
- embed_gradient: float32 [192, 256], replicated
- norm_gradient: float32 [256], replicated
- attend_gradient: float32 [256, 768], replicated
- output_gradient: float32 [256, 256], replicated
- second_gradient: float32 [256], replicated
- expand_gradient: float32 [256, 512], replicated
- reduce_gradient: float32 [512, 256], replicated
- decode_gradient: float32 [256, 192], replicated
All inputs are finite; a program needn't handle non-finite values.
Results may differ from a plain program's by a relative error of at most 0.0001.
Values sent between devices are 32-bit elements; how exact they have to be, the bound alone decides.
No kernel may reach another device: no remote copies, remote signals or barrier semaphores. Data moves between devices by JAX's collectives and lax.ppermute only.
A program may use at most 128 MiB of HBM per device.

v0:
```python
import jax
import jax.numpy as jnp
from jax import lax
from jax.sharding import PartitionSpec as P

PATCH = 4
HEADS = 8
STEPS = 2
EXACT = lax.Precision.HIGHEST
EPSILON = 1e-06
TIME_STEP = 0.1
VISCOSITY = 0.5


def with_halo(x, sides, width):
    for axis, dim in sides:
        count, length = (lax.axis_size(axis), x.shape[dim])
        up = [(i, (i + 1) % count) for i in range(count)]
        down = [(j, i) for i, j in up]
        last = lax.slice_in_dim(x, length - width, length, axis=dim)
        leading = lax.slice_in_dim(x, 0, width, axis=dim)
        before = lax.ppermute(last, axis, up)
        after = lax.ppermute(leading, axis, down)
        x = jnp.concatenate([before, x, after], axis=dim)
    return x


def matmul(left, right):
    return jnp.dot(left, right, precision=EXACT)


def rms_scale(values, gain):
    power = jnp.mean(values * values, axis=-1, keepdims=True)
    return values * lax.rsqrt(power + EPSILON) * gain


def closure(ext, params):
    (
        embed_weight,
        norm_gain,
        attend_weight,
        output_weight,
        second_gain,
        expand_weight,
        reduce_weight,
        decode_weight,
    ) = params
    wide, tall, depth = ext.shape
    levels = depth // 3
    across, along, upward = (wide // PATCH, tall // PATCH, levels // PATCH)
    patches = ext.reshape(across, PATCH, along, PATCH, 3, upward, PATCH).transpose(
        0, 2, 5, 4, 1, 3, 6
    )
    patches = patches.reshape(across, along, upward, 3 * PATCH * PATCH * PATCH)
    tokens = matmul(patches, embed_weight)
    width = tokens.shape[-1]
    head_size = width // HEADS
    mixed = matmul(rms_scale(tokens, norm_gain), attend_weight)
    inner_x, inner_y = (across - 2, along - 2)
    queries = mixed[1:-1, 1:-1, :, :width].reshape(inner_x, inner_y, upward, HEADS, head_size)
    keyset = mixed[:, :, :, width : 2 * width]
    valset = mixed[:, :, :, 2 * width :]
    offsets = [(shift_x, shift_y) for shift_x in range(3) for shift_y in range(3)]
    keyblock = jnp.concatenate(
        [keyset[sx : sx + inner_x, sy : sy + inner_y] for sx, sy in offsets], axis=2
    )
    valblock = jnp.concatenate(
        [valset[sx : sx + inner_x, sy : sy + inner_y] for sx, sy in offsets], axis=2
    )
    keyblock = keyblock.reshape(inner_x, inner_y, 9 * upward, HEADS, head_size)
    valblock = valblock.reshape(inner_x, inner_y, 9 * upward, HEADS, head_size)
    factor = head_size ** (-0.5)
    scores = jnp.einsum("xyzhe,xywhe->xyhzw", queries, keyblock, precision=EXACT) * factor
    weights = jnp.exp(scores)
    weights = weights / jnp.sum(weights, axis=-1, keepdims=True)
    attended = jnp.einsum("xyhzw,xywhe->xyzhe", weights, valblock, precision=EXACT)
    attended = attended.reshape(inner_x, inner_y, upward, width)
    middle = tokens[1:-1, 1:-1] + matmul(attended, output_weight)
    hidden = jax.nn.silu(matmul(rms_scale(middle, second_gain), expand_weight))
    middle = middle + matmul(hidden, reduce_weight)
    result = matmul(middle, decode_weight).reshape(inner_x, inner_y, upward, 3, PATCH, PATCH, PATCH)
    return result.transpose(0, 4, 1, 5, 3, 2, 6).reshape(inner_x * PATCH, inner_y * PATCH, depth)


def advance(ext, params):
    wide, tall, depth = ext.shape
    levels = depth // 3
    inner = ext[PATCH : wide - PATCH, PATCH : tall - PATCH]
    east = ext[PATCH + 1 : wide - PATCH + 1, PATCH : tall - PATCH]
    west = ext[PATCH - 1 : wide - PATCH - 1, PATCH : tall - PATCH]
    north = ext[PATCH : wide - PATCH, PATCH + 1 : tall - PATCH + 1]
    south = ext[PATCH : wide - PATCH, PATCH - 1 : tall - PATCH - 1]
    level = jnp.arange(depth, dtype=jnp.int32) % levels
    blank = jnp.zeros(inner.shape[:2] + (1,), jnp.float32)
    upper = jnp.where(level == levels - 1, 0.0, jnp.concatenate([inner[:, :, 1:], blank], axis=2))
    lower = jnp.where(level == 0, 0.0, jnp.concatenate([blank, inner[:, :, :-1]], axis=2))
    laplace = east + west + north + south + upper + lower - 6.0 * inner
    speed_x = jnp.concatenate([inner[:, :, 0:levels]] * 3, axis=2)
    speed_y = jnp.concatenate([inner[:, :, levels : 2 * levels]] * 3, axis=2)
    speed_z = jnp.concatenate([inner[:, :, 2 * levels :]] * 3, axis=2)
    carried = 0.5 * (
        speed_x * (east - west) + speed_y * (north - south) + speed_z * (upper - lower)
    )
    return inner + TIME_STEP * (VISCOSITY * laplace - carried + closure(ext, params))


def fold(spread, margin):
    for axis_dim in (0, 1):
        length = spread.shape[axis_dim] - 4 * margin
        middle = lax.slice_in_dim(spread, 2 * margin, 2 * margin + length, axis=axis_dim)
        lowside = lax.slice_in_dim(spread, 0, margin, axis=axis_dim)
        highside = lax.slice_in_dim(spread, length + 3 * margin, length + 4 * margin, axis=axis_dim)
        pad_low = [(0, 0), (0, 0), (0, 0)]
        pad_high = [(0, 0), (0, 0), (0, 0)]
        pad_low[axis_dim] = (0, length - margin)
        pad_high[axis_dim] = (length - margin, 0)
        spread = middle + jnp.pad(lowside, pad_low) + jnp.pad(highside, pad_high)
    return spread


def shards(
    field,
    target,
    embed_weight,
    norm_gain,
    attend_weight,
    output_weight,
    second_gain,
    expand_weight,
    reduce_weight,
    decode_weight,
):
    params = (
        embed_weight,
        norm_gain,
        attend_weight,
        output_weight,
        second_gain,
        expand_weight,
        reduce_weight,
        decode_weight,
    )
    energy = lax.psum(jnp.sum(target * target), ("gx", "gy"))
    current = field
    pullbacks = []
    for step in range(STEPS):
        extended = with_halo(current, (("gx", 0), ("gy", 1)), PATCH)
        current, pullback = jax.vjp(advance, extended, params)
        pullbacks.append(pullback)
    residue = current - target
    cotangent = 2.0 * residue
    gradients = None
    for pullback in reversed(pullbacks):
        back_ext, back_params = pullback(cotangent)
        gradients = (
            back_params if gradients is None else jax.tree.map(jnp.add, gradients, back_params)
        )
        spread = with_halo(back_ext, (("gx", 0), ("gy", 1)), PATCH)
        cotangent = fold(spread, PATCH)
    local_misfit = jnp.sum(residue * residue)
    misfit = lax.psum(local_misfit, ("gx", "gy"))
    summed = lax.psum(tuple(gradients), ("gx", "gy"))
    entries = (
        field.shape[0] * lax.axis_size("gx") * field.shape[1] * lax.axis_size("gy") * field.shape[2]
    )
    scale = jnp.float32(entries) / energy
    loss = misfit / energy
    return (loss, scale * cotangent) + tuple((scale * piece for piece in summed))


def solution(mesh):
    in_specs = (P("gx", "gy", None), P("gx", "gy", None), P(), P(), P(), P(), P(), P(), P(), P())
    out_specs = (P(), P("gx", "gy", None), P(), P(), P(), P(), P(), P(), P(), P())
    return jax.shard_map(shards, mesh=mesh, in_specs=in_specs, out_specs=out_specs, check_vma=False)
```

profile of v0, /device:TPU:1, one launch (start us, length us, event | category | flops | bytes accessed | tf_op | source)
XLA Modules:
  0.0 810.8 jit_solution(4378260794345569212)
XLA Ops:
  8.1 12.9 %collective-permute-start = (f32[4,8,192]{2,1,0:T(8,128)S(1)}, f32[4,8,192]{2,1,0:T(8,128)S(1)}, u32[]{:S(2)}, u32[]{:S(2)}) collective-permute-start(f32[4,8,192]{2,1,0:T(8,128)S(1)} %get-tuple-element.154), channel_id=1, source_target_pairs={{16,0},{32,16},{48,32},{64,48},{80,64},{96,80},{112,96},{128,112},... | collective-permute-start | bytes 73736 | tf_op jit(solution)/shard_map/ppermute | solution.py:23
  29.2 6.3 collective-permute-start.3
  38.2 4.5 collective-permute-done.2
  43.3 5.0 reshape.216
  48.4 6.5 copy.78
  74.2 5.5 collective-permute-start.4
  86.4 4.5 collective-permute-done.6
  90.9 5.0 reshape.224
  96.0 7.0 copy.86
  103.0 3.9 multiply_reduce_fusion.6
  154.1 3.2 fusion.169
  191.8 6.1 copy.118
  198.1 5.1 reshape.239
  205.6 5.6 collective-permute-start.9
  212.6 3.2 collective-permute-start.10
  215.8 4.0 collective-permute-start.11
  262.6 3.3 fusion.168
  293.5 6.3 copy.143
  299.8 5.0 reshape.247
  307.9 5.5 collective-permute-start.13
  313.4 107.6 %all-reduce.72 = (f32[]{:T(128)}, f32[]{:T(128)}, f32[256]{0:T(256)S(1)}, f32[256]{0:T(256)S(1)}) all-reduce(f32[]{:T(128)} %get-tuple-element.141, f32[]{:T(128)} %multiply_reduce_fusion.12, f32[256]{0:T(256)S(1)} %add.385, f32[256]{0:T(256)S(1)} %add.388), channel_id=1, replica_groups=mesh['gx'=32,'gy'=16] {'gx','gy'}, use_global_device_ids=true, to_apply=%region_7.8 | all-reduce | flops 514 | bytes 4112 | tf_op jit(solution)/shard_map/psum | solution.py:161
  422.3 3.5 collective-permute-start.14
  429.7 3.6 collective-permute-done.15
  434.2 360.8 %all-reduce.76.cloned.1.call-done = (f32[192,256]{1,0:T(8,128)}, f32[256,768]{1,0:T(8,128)}, f32[256,256]{1,0:T(8,128)}, f32[256,512]{1,0:T(8,128)}, f32[512,256]{1,0:T(8,128)}, /*index=5*/f32[256,192]{0,1:T(8,128)}) async-done(((f32[192,256]{1,0:T(8,128)}, f32[256,768]{1,0:T(8,128)}, f32[256,256]{1,0:T(8,128)}, f32[256,512]{1,0:T(8,128)}, f32[512,256]{1,0:T(8,128)}, /*index=5*/f32[256,192]{0,1:T(8,128)}), ...) | async-done | bytes 2490384 | tf_op jit(solution)/shard_map/psum | solution.py:162
  (632 shorter events, 206.8 us)
Async XLA Ops:
  7.2 51.0 %copy-start = (f32[256,768]{1,0:T(8,128)S(1)}, f32[256,768]{1,0:T(8,128)}, u32[]{:S(2)}) copy-start(f32[256,768]{1,0:T(8,128)} %param.14) | copy-start | bytes 2359300
  7.2 787.8 %all-reduce.76.cloned.1.call-start = ((), (), s32[]{:S(2)}) async-start(), calls=%async_computation | async-start | bytes 4980736 | tf_op jit(solution)/shard_map/psum | solution.py:162
  8.1 20.5 %collective-permute-start = (f32[4,8,192]{2,1,0:T(8,128)S(1)}, f32[4,8,192]{2,1,0:T(8,128)S(1)}, u32[]{:S(2)}, u32[]{:S(2)}) collective-permute-start(f32[4,8,192]{2,1,0:T(8,128)S(1)} %get-tuple-element.154), channel_id=1, source_target_pairs={{16,0},{32,16},{48,32},{64,48},{80,64},{96,80},{112,96},{128,112},... | collective-permute-start | bytes 73736 | tf_op jit(solution)/shard_map/ppermute | solution.py:23
  20.9 6.8 collective-permute-start.1
  29.2 9.0 %collective-permute-start.3 = (f32[16,4,192]{2,1,0:T(4,128)S(1)}, f32[16,4,192]{2,1,0:T(4,128)S(1)}, u32[]{:S(2)}, u32[]{:S(2)}) collective-permute-start(f32[16,4,192]{2,1,0:T(4,128)S(1)} %get-tuple-element.122), channel_id=1, source_target_pairs={{0,1},{1,2},{2,3},{3,4},{4,5},{5,6},{6,7},{7,8},{8,9},{9,10},{10,1... | collective-permute-start | bytes 147464 | tf_op jit(solution)/shard_map/ppermute | solution.py:22
  35.5 7.1 collective-permute-start.2
  37.5 33.5 %copy-start.191 = (pred[192]{0:T(512)(128)(4,1)}, pred[192]{0:T(512)(128)(4,1)S(1)}, u32[]{:S(2)}) copy-start(pred[192]{0:T(512)(128)(4,1)S(1)} %get-tuple-element.177) | copy-start | bytes 580
  37.5 33.5 %copy-start.196 = (pred[192]{0:T(512)(128)(4,1)}, pred[192]{0:T(512)(128)(4,1)S(1)}, u32[]{:S(2)}) copy-start(pred[192]{0:T(512)(128)(4,1)S(1)} %get-tuple-element.176) | copy-start | bytes 580
  72.3 8.1 %collective-permute-start.5 = (f32[4,8,192]{2,1,0:T(8,128)S(1)}, f32[4,8,192]{2,1,0:T(8,128)S(1)}, u32[]{:S(2)}, u32[]{:S(2)}) collective-permute-start(f32[4,8,192]{2,1,0:T(8,128)S(1)} %get-tuple-element.147), channel_id=1, source_target_pairs={{0,16},{16,32},{32,48},{48,64},{64,80},{80,96},{96,112},{112,128},... | collective-permute-start | bytes 73736 | tf_op jit(solution)/shard_map/ppermute | solution.py:22
  74.2 6.5 collective-permute-start.4
  80.7 5.6 collective-permute-start.7
  83.7 7.1 collective-permute-start.6
  203.2 16.6 %copy-start.155 = (f32[2,2,8,16]{3,2,1,0:T(8,128)S(1)}, f32[2,2,8,16]{3,2,1,0:T(8,128)}, u32[]{:S(2)}) copy-start(f32[2,2,8,16]{3,2,1,0:T(8,128)} %copy-done.154) | copy-start | bytes 6148
  203.5 20.1 %copy-start.194 = (pred[8]{0:T(512)(128)(4,1)S(1)}, pred[8]{0:T(512)(128)(4,1)}, u32[]{:S(2)}) copy-start(pred[8]{0:T(512)(128)(4,1)} %constant.73.clone.1) | copy-start | bytes 28
  203.7 20.0 %copy-start.108 = (f32[8,8,64]{2,1,0:T(8,128)S(1)}, f32[8,8,64]{2,1,0:T(8,128)}, u32[]{:S(2)}) copy-start(f32[8,8,64]{2,1,0:T(8,128)} %get-tuple-element.152) | copy-start | bytes 49156
  203.7 8.3 %collective-permute-start.8 = (f32[4,16,192]{2,1,0:T(8,128)S(1)}, f32[4,16,192]{2,1,0:T(8,128)S(1)}, u32[]{:S(2)}, u32[]{:S(2)}) collective-permute-start(f32[4,16,192]{2,1,0:T(8,128)S(1)} %get-tuple-element.112), channel_id=1, source_target_pairs={{0,16},{16,32},{32,48},{48,64},{64,80},{80,96},{96,112},{112,128},... | collective-permute-start | bytes 147464 | tf_op jit(solution)/shard_map/ppermute | solution.py:22
  205.6 6.9 collective-permute-start.9
  212.6 7.8 collective-permute-start.10
  215.8 7.7 collective-permute-start.11
  305.2 128.2 %copy-start.195 = (pred[8]{0:T(512)(128)(4,1)S(1)}, pred[8]{0:T(512)(128)(4,1)}, u32[]{:S(2)}) copy-start(pred[8]{0:T(512)(128)(4,1)} %constant.73.clone.1) | copy-start | bytes 28
  306.0 116.3 %collective-permute-start.12 = (f32[4,16,192]{2,1,0:T(8,128)S(1)}, f32[4,16,192]{2,1,0:T(8,128)S(1)}, u32[]{:S(2)}, u32[]{:S(2)}) collective-permute-start(f32[4,16,192]{2,1,0:T(8,128)S(1)} %get-tuple-element.110), channel_id=1, source_target_pairs={{0,16},{16,32},{32,48},{48,64},{64,80},{80,96},{96,112},{112,128},... | collective-permute-start | bytes 147464 | tf_op jit(solution)/shard_map/ppermute | solution.py:22
  307.9 114.4 %collective-permute-start.13 = (f32[4,16,192]{2,1,0:T(8,128)S(1)}, f32[4,16,192]{2,1,0:T(8,128)S(1)}, u32[]{:S(2)}, u32[]{:S(2)}) collective-permute-start(f32[4,16,192]{2,1,0:T(8,128)S(1)} %get-tuple-element.111), channel_id=1, source_target_pairs={{16,0},{32,16},{48,32},{64,48},{80,64},{96,80},{112,96},{128,112},... | collective-permute-start | bytes 147464 | tf_op jit(solution)/shard_map/ppermute | solution.py:23
  422.3 7.4 collective-permute-start.14
  425.9 7.4 collective-permute-start.15
  (197 other events, 830.2 us)
Sparse Core Ops, SparseCore 0:
  305.3 489.6 all-reduce.75
where the time goes:
time: 823 us; the launch traced here: 811 us
  waiting for transfers between devices  379 us (46%)
  local copies, waits for them, and re-layouts  147 us (18%)
  blocking collectives  108 us (13%)
  matrix products  67.6 us (8%)
  starting transfers between devices  63 us (8%)
  other arithmetic  26.2 us (3%)
  between operations  20.3 us (2%)
    psum x1, waiting for transfers between devices, shards(): summed = lax.psum(tuple(gradients), ('gx', 'gy'))  361 us
    psum x1, blocking collectives, shards(): misfit = lax.psum(local_misfit, ('gx', 'gy'))  108 us
    unnamed x462, local copies, waits for them, and re-layouts  58.7 us
    dot_general x36, matrix products, matmul(): return jnp.dot(left, right, precision=EXACT)  49.2 us
    ppermute x8, starting transfers between devices, with_halo(): after = lax.ppermute(leading, axis, down)  39.2 us
    transpose x4, local copies, waits for them, and re-layouts, closure(): ext.reshape(across, PATCH, along, PATCH, 3, upward, PATCH)  25.9 us
    ppermute x8, starting transfers between devices, with_halo(): before = lax.ppermute(last, axis, up)  23.7 us
    reshape x4, local copies, waits for them, and re-layouts, closure(): ext.reshape(across, PATCH, along, PATCH, 3, upward, PATCH)  20.2 us
  transfers between devices with their start and end apart: 17, of which 8 were waited for; matrix products, arithmetic and copies ran while one was open for 1% of the time, Pallas kernels for 0%

commit v1 on v0

--- a/solution.py
+++ b/solution.py
@@ -159,7 +159,8 @@
         cotangent = fold(spread, PATCH)
     local_misfit = jnp.sum(residue * residue)
     misfit = lax.psum(local_misfit, ("gx", "gy"))
-    summed = lax.psum(tuple(gradients), ("gx", "gy"))
+    half = lax.psum(tuple(gradients), "gy")
+    summed = lax.psum(half, "gx")
     entries = (
         field.shape[0] * lax.axis_size("gx") * field.shape[1] * lax.axis_size("gy") * field.shape[2]
     )

time: 823 us -> 760 us (0.923)
  the two profiles are of different devices: /device:TPU:1 before, /device:TPU:16 now
where the time goes in v1:
time: 760 us; the launch traced here: 748 us
  waiting for transfers between devices  236 us (31%)
  blocking collectives  198 us (26%)
  local copies, waits for them, and re-layouts  147 us (19%)
  matrix products  65.8 us (9%)
  starting transfers between devices  53.6 us (7%)
  other arithmetic  27 us (4%)
  between operations  20.4 us (3%)
    psum x1, waiting for transfers between devices, shards(): summed = lax.psum(half, 'gx')  171 us
    psum x1, blocking collectives, shards(): misfit = lax.psum(local_misfit, ('gx', 'gy'))  103 us
    psum x1, blocking collectives, shards(): summed = lax.psum(half, 'gx')  63.7 us
    unnamed x462, local copies, waits for them, and re-layouts  60.1 us
    dot_general x36, matrix products, matmul(): return jnp.dot(left, right, precision=EXACT)  48.3 us
    psum x1, waiting for transfers between devices, shards(): half = lax.psum(tuple(gradients), 'gy')  35.4 us
    ppermute x8, starting transfers between devices, with_halo(): after = lax.ppermute(leading, axis, down)  32.2 us
    psum x1, blocking collectives, shards(): half = lax.psum(tuple(gradients), 'gy')  31.7 us
  transfers between devices with their start and end apart: 18, of which 9 were waited for; matrix products, arithmetic and copies ran while one was open for 3% of the time, Pallas kernels for 0%

profile of v1, /device:TPU:16, one launch (start us, length us, event | category | flops | bytes accessed | tf_op | source)
XLA Modules:
  0.0 748.4 jit_solution(15056238327043706316)
XLA Ops:
  11.5 10.9 %collective-permute-start = (f32[4,8,192]{2,1,0:T(8,128)S(1)}, f32[4,8,192]{2,1,0:T(8,128)S(1)}, u32[]{:S(2)}, u32[]{:S(2)}) collective-permute-start(f32[4,8,192]{2,1,0:T(8,128)S(1)} %get-tuple-element.162), channel_id=1, source_target_pairs={{16,0},{32,16},{48,32},{64,48},{80,64},{96,80},{112,96},{128,112},... | collective-permute-start | bytes 73736 | tf_op jit(solution)/shard_map/ppermute | solution.py:23
  27.0 3.7 collective-permute-start.2
  33.3 5.4 collective-permute-done.3
  39.3 5.1 reshape.216
  44.4 6.5 copy.78
  77.0 4.4 collective-permute-done.5
  86.5 4.9 collective-permute-done.7
  91.5 5.1 reshape.224
  96.5 7.0 copy.86
  103.5 3.9 multiply_reduce_fusion.6
  191.1 6.3 copy.118
  197.5 5.1 reshape.239
  205.3 3.8 collective-permute-start.8
  209.8 3.9 collective-permute-done.8
  218.9 5.1 collective-permute-done.10
  291.9 102.7 %all-reduce.72 = (f32[]{:T(128)}, f32[]{:T(128)}) all-reduce(f32[]{:T(128)} %get-tuple-element.149, f32[]{:T(128)} %multiply_reduce_fusion.12), channel_id=1, replica_groups=mesh['gx'=32,'gy'=16] {'gx','gy'}, use_global_device_ids=true, to_apply=%region_7.8 | all-reduce | flops 2 | bytes 16 | tf_op jit(solution)/shard_map/psum | solution.py:161
  398.1 6.3 copy.143
  404.4 5.0 reshape.247
  409.5 35.4 %all-reduce.82.cloned.1.call-done = (f32[192,256]{1,0:T(8,128)}, f32[256,768]{1,0:T(8,128)}, f32[256,256]{1,0:T(8,128)}, f32[256,512]{1,0:T(8,128)}, f32[512,256]{1,0:T(8,128)}, /*index=5*/f32[256,192]{0,1:T(8,128)}) async-done(((f32[192,256]{1,0:T(8,128)}, f32[256,768]{1,0:T(8,128)}, f32[256,256]{1,0:T(8,128)}, f32[256,512]{1,0:T(8,128)}, f32[512,256]{1,0:T(8,128)}, /*index=5*/f32[256,192]{0,1:T(8,128)}), ...) | async-done | bytes 2490384 | tf_op jit(solution)/shard_map/psum | solution.py:162
  446.0 6.8 collective-permute-start.13
  454.8 31.7 %all-reduce.75 = (f32[256]{0:T(256)S(1)}, f32[256]{0:T(256)S(1)}) all-reduce(f32[256]{0:T(256)S(1)} %add.401, f32[256]{0:T(256)S(1)} %add.404), channel_id=1, replica_groups=mesh['gx'=32,'gy'=16] {'gy'}, use_global_device_ids=true, to_apply=%region_20.21 | all-reduce | flops 512 | bytes 4096 | tf_op jit(solution)/shard_map/psum | solution.py:162
  486.5 63.7 %all-reduce.73 = (f32[256]{0:T(256)S(1)}, f32[256]{0:T(256)S(1)}) all-reduce(f32[256]{0:T(256)S(1)} %get-tuple-element.28, f32[256]{0:T(256)S(1)} %get-tuple-element.29), channel_id=1, replica_groups=mesh['gx'=32,'gy'=16] {'gx'}, use_global_device_ids=true, to_apply=%region_21.22 | all-reduce | flops 512 | bytes 4096 | tf_op jit(solution)/shard_map/psum | solution.py:163
  555.7 6.1 collective-permute-done.14
  562.8 170.6 %all-reduce.80.cloned.1.call-done = (f32[192,256]{1,0:T(8,128)}, f32[256,768]{1,0:T(8,128)}, f32[256,256]{1,0:T(8,128)}, f32[256,512]{1,0:T(8,128)}, f32[512,256]{1,0:T(8,128)}, /*index=5*/f32[256,192]{0,1:T(8,128)}) async-done(((f32[192,256]{1,0:T(8,128)}, f32[256,768]{1,0:T(8,128)}, f32[256,256]{1,0:T(8,128)}, f32[256,512]{1,0:T(8,128)}, f32[512,256]{1,0:T(8,128)}, /*index=5*/f32[256,192]{0,1:T(8,128)}), ...) | async-done | bytes 2490384 | tf_op jit(solution)/shard_map/psum | solution.py:163
  (637 shorter events, 219.0 us)
Async XLA Ops:
  7.2 47.1 %copy-start = (f32[256,768]{1,0:T(8,128)S(1)}, f32[256,768]{1,0:T(8,128)}, u32[]{:S(2)}) copy-start(f32[256,768]{1,0:T(8,128)} %param.14) | copy-start | bytes 2359300
  7.2 437.7 %all-reduce.82.cloned.1.call-start = ((), (), s32[]{:S(2)}) async-start(), calls=%async_computation.1 | async-start | bytes 4980736 | tf_op jit(solution)/shard_map/psum | solution.py:162
  8.1 17.4 %collective-permute-start.1 = (f32[4,8,192]{2,1,0:T(8,128)S(1)}, f32[4,8,192]{2,1,0:T(8,128)S(1)}, u32[]{:S(2)}, u32[]{:S(2)}) collective-permute-start(f32[4,8,192]{2,1,0:T(8,128)S(1)} %get-tuple-element.163), channel_id=1, source_target_pairs={{0,16},{16,32},{32,48},{48,64},{64,80},{80,96},{96,112},{112,128},... | collective-permute-start | bytes 73736 | tf_op jit(solution)/shard_map/ppermute | solution.py:22
  11.5 14.9 %collective-permute-start = (f32[4,8,192]{2,1,0:T(8,128)S(1)}, f32[4,8,192]{2,1,0:T(8,128)S(1)}, u32[]{:S(2)}, u32[]{:S(2)}) collective-permute-start(f32[4,8,192]{2,1,0:T(8,128)S(1)} %get-tuple-element.162), channel_id=1, source_target_pairs={{16,0},{32,16},{48,32},{64,48},{80,64},{96,80},{112,96},{128,112},... | collective-permute-start | bytes 73736 | tf_op jit(solution)/shard_map/ppermute | solution.py:23
  27.0 6.3 collective-permute-start.2
  30.6 8.0 %collective-permute-start.3 = (f32[16,4,192]{2,1,0:T(4,128)S(1)}, f32[16,4,192]{2,1,0:T(4,128)S(1)}, u32[]{:S(2)}, u32[]{:S(2)}) collective-permute-start(f32[16,4,192]{2,1,0:T(4,128)S(1)} %get-tuple-element.130), channel_id=1, source_target_pairs={{0,1},{1,2},{2,3},{3,4},{4,5},{5,6},{6,7},{7,8},{8,9},{9,10},{10,1... | collective-permute-start | bytes 147464 | tf_op jit(solution)/shard_map/ppermute | solution.py:22
  32.6 36.6 %copy-start.191 = (pred[192]{0:T(512)(128)(4,1)}, pred[192]{0:T(512)(128)(4,1)S(1)}, u32[]{:S(2)}) copy-start(pred[192]{0:T(512)(128)(4,1)S(1)} %get-tuple-element.185) | copy-start | bytes 580
  32.6 36.6 %copy-start.196 = (pred[192]{0:T(512)(128)(4,1)}, pred[192]{0:T(512)(128)(4,1)S(1)}, u32[]{:S(2)}) copy-start(pred[192]{0:T(512)(128)(4,1)S(1)} %get-tuple-element.184) | copy-start | bytes 580
  70.5 6.6 collective-permute-start.4
  73.5 7.9 %collective-permute-start.5 = (f32[4,8,192]{2,1,0:T(8,128)S(1)}, f32[4,8,192]{2,1,0:T(8,128)S(1)}, u32[]{:S(2)}, u32[]{:S(2)}) collective-permute-start(f32[4,8,192]{2,1,0:T(8,128)S(1)} %get-tuple-element.155), channel_id=1, source_target_pairs={{0,16},{16,32},{32,48},{48,64},{64,80},{80,96},{96,112},{112,128},... | collective-permute-start | bytes 73736 | tf_op jit(solution)/shard_map/ppermute | solution.py:22
  81.5 5.0 collective-permute-start.6
  83.4 8.0 %collective-permute-start.7 = (f32[16,4,192]{2,1,0:T(4,128)S(1)}, f32[16,4,192]{2,1,0:T(4,128)S(1)}, u32[]{:S(2)}, u32[]{:S(2)}) collective-permute-start(f32[16,4,192]{2,1,0:T(4,128)S(1)} %get-tuple-element.128), channel_id=1, source_target_pairs={{0,1},{1,2},{2,3},{3,4},{4,5},{5,6},{6,7},{7,8},{8,9},{9,10},{10,1... | collective-permute-start | bytes 147464 | tf_op jit(solution)/shard_map/ppermute | solution.py:22
  203.1 6.7 collective-permute-start.9
  205.3 8.4 %collective-permute-start.8 = (f32[4,16,192]{2,1,0:T(8,128)S(1)}, f32[4,16,192]{2,1,0:T(8,128)S(1)}, u32[]{:S(2)}, u32[]{:S(2)}) collective-permute-start(f32[4,16,192]{2,1,0:T(8,128)S(1)} %get-tuple-element.120), channel_id=1, source_target_pairs={{0,16},{16,32},{32,48},{48,64},{64,80},{80,96},{96,112},{112,128},... | collective-permute-start | bytes 147464 | tf_op jit(solution)/shard_map/ppermute | solution.py:22
  213.7 5.2 collective-permute-start.11
  215.7 8.3 %collective-permute-start.10 = (f32[24,4,192]{2,1,0:T(4,128)S(1)}, f32[24,4,192]{2,1,0:T(4,128)S(1)}, u32[]{:S(2)}, u32[]{:S(2)}) collective-permute-start(f32[24,4,192]{2,1,0:T(4,128)S(1)} %get-tuple-element.116), channel_id=1, source_target_pairs={{0,1},{1,2},{2,3},{3,4},{4,5},{5,6},{6,7},{7,8},{8,9},{9,10},{10,1... | collective-permute-start | bytes 221192 | tf_op jit(solution)/shard_map/ppermute | solution.py:22
  289.9 106.7 %copy-start.35 = (f32[192,256]{1,0:T(8,128)S(1)}, f32[192,256]{1,0:T(8,128)}, u32[]{:S(2)}) copy-start(f32[192,256]{1,0:T(8,128)} %param.12) | copy-start | bytes 589828
  289.9 106.7 %copy-start.175 = (f32[256]{0:T(256)S(1)}, f32[256]{0:T(256)}, u32[]{:S(2)}) copy-start(f32[256]{0:T(256)} %param.13) | copy-start | bytes 3076
  291.3 442.1 %all-reduce.80.cloned.1.call-start = ((), (), s32[]{:S(2)}) async-start(), calls=%async_computation | async-start | bytes 4980736 | tf_op jit(solution)/shard_map/psum | solution.py:163
  445.9 116.1 %copy-start.195 = (pred[8]{0:T(512)(128)(4,1)S(1)}, pred[8]{0:T(512)(128)(4,1)}, u32[]{:S(2)}) copy-start(pred[8]{0:T(512)(128)(4,1)} %constant.73.clone.1) | copy-start | bytes 28
  446.0 104.8 %collective-permute-start.13 = (f32[4,16,192]{2,1,0:T(8,128)S(1)}, f32[4,16,192]{2,1,0:T(8,128)S(1)}, u32[]{:S(2)}, u32[]{:S(2)}) collective-permute-start(f32[4,16,192]{2,1,0:T(8,128)S(1)} %get-tuple-element.119), channel_id=1, source_target_pairs={{16,0},{32,16},{48,32},{64,48},{80,64},{96,80},{112,96},{128,112},... | collective-permute-start | bytes 147464 | tf_op jit(solution)/shard_map/ppermute | solution.py:23
  452.8 98.0 %collective-permute-start.12 = (f32[4,16,192]{2,1,0:T(8,128)S(1)}, f32[4,16,192]{2,1,0:T(8,128)S(1)}, u32[]{:S(2)}, u32[]{:S(2)}) collective-permute-start(f32[4,16,192]{2,1,0:T(8,128)S(1)} %get-tuple-element.118), channel_id=1, source_target_pairs={{0,16},{16,32},{32,48},{48,64},{64,80},{80,96},{96,112},{112,128},... | collective-permute-start | bytes 147464 | tf_op jit(solution)/shard_map/ppermute | solution.py:22
  550.8 4.9 collective-permute-start.15
  552.8 9.1 %collective-permute-start.14 = (f32[24,4,192]{2,1,0:T(4,128)S(1)}, f32[24,4,192]{2,1,0:T(4,128)S(1)}, u32[]{:S(2)}, u32[]{:S(2)}) collective-permute-start(f32[24,4,192]{2,1,0:T(4,128)S(1)} %get-tuple-element.114), channel_id=1, source_target_pairs={{0,1},{1,2},{2,3},{3,4},{4,5},{5,6},{6,7},{7,8},{8,9},{9,10},{10,1... | collective-permute-start | bytes 221192 | tf_op jit(solution)/shard_map/ppermute | solution.py:22
  (198 other events, 1091.1 us)
Sparse Core Ops, SparseCore 0:
  291.4 153.4 all-reduce.81
  448.3 284.9 all-reduce.79
